TPU v7x, 32 devices: a whole 2x2x4 slice. The times are simulated.
32 devices in a mesh: dp: 8 (over z, core), tensor: 4 (over y, x).
Axes of the slice: x: 2, y: 2, z: 4, core: 2. Of those that a mesh axis runs over, the one named last changes fastest.
Arguments:
- block_input: bfloat16 [4096, 2048], P('dp'), may hold values from -6 to 6
- cotangent: bfloat16 [4096, 2048], P('dp'), may hold values from -6 to 6
- lengths: int32 [8], P('dp'), may hold values from 1 to 512, as said below
- attn_gain: bfloat16 [2048], P('dp'), may hold values from 0.5 to 1.5
- attn_shift: bfloat16 [2048], P('dp'), may hold values from -3 to 3
- ffn_gain: bfloat16 [2048], P('dp'), may hold values from 0.5 to 1.5
- ffn_shift: bfloat16 [2048], P('dp'), may hold values from -3 to 3
- qkv_weight: bfloat16 [3, 2048, 2048], P(None, 'dp', 'tensor')
- qkv_bias: bfloat16 [3, 2048], P(None, ('tensor', 'dp')), may hold values from -3 to 3
- out_weight: bfloat16 [2048, 2048], P('tensor', 'dp'), may hold values from -1 to 1
- out_bias: bfloat16 [2048], P('dp'), may hold values from -3 to 3
- up_weight: bfloat16 [2048, 8192], P('dp', 'tensor'), may hold values from -0.125 to 0.125
- up_bias: bfloat16 [8192], P(('tensor', 'dp')), may hold values from -3 to 3
- down_weight: bfloat16 [8192, 2048], P('tensor', 'dp'), may hold values from -0.0625 to 0.0625
Outputs:
- block_output: bfloat16 [4096, 2048], P('dp')
- dblock_input: bfloat16 [4096, 2048], P('dp')
- dattn_gain: float32 [2048], P('dp')
- dattn_shift: float32 [2048], P('dp')
- dffn_gain: float32 [2048], P('dp')
- dffn_shift: float32 [2048], P('dp')
- dqkv_weight: float32 [3, 2048, 2048], P(None, 'dp', 'tensor')
- dqkv_bias: float32 [3, 2048], P(None, ('tensor', 'dp'))
- dout_weight: float32 [2048, 2048], P('tensor', 'dp')
- dout_bias: float32 [2048], P('dp')
- dup_weight: float32 [2048, 8192], P('dp', 'tensor')
- dup_bias: float32 [8192], P(('tensor', 'dp'))
- ddown_weight: float32 [8192, 2048], P('tensor', 'dp')
Inputs may be any that keep to these rules, and one draw needn't show every extreme that they name: `lengths`: one sequence for each index of dp; some sequence uses all 512 slots.
All inputs are finite; a program needn't handle non-finite values.
Results may differ from a plain program's by a relative error of at most 0.014.
Values may be sent and summed in bfloat16 or wider, within the bound.
A program may use at most 192 MiB of HBM per device.

v0:
```python
import math
import jax
import jax.numpy as jnp
from jax import lax
from jax.sharding import PartitionSpec as P

HD = 256
ROT = 64
norm_eps = 1e-05
rope_base = 10000.0


def rope_tables(row_count, rot_width):
    half_rot = rot_width // 2
    freq_idx = jnp.arange(half_rot, dtype=jnp.float32)
    inv_freq = jnp.exp(-(2.0 * freq_idx / rot_width) * math.log(rope_base))
    angles = jnp.arange(row_count, dtype=jnp.float32)[:, None] * inv_freq[None, :]
    return (jnp.cos(angles), jnp.sin(angles))


def rotate(heads_arr, cosine, sine_tab, direction):
    half_rot = ROT // 2
    first_half = heads_arr[..., :half_rot]
    second_half = heads_arr[..., half_rot:ROT]
    rest_dims = heads_arr[..., ROT:]
    cos_b = cosine[:, None, :]
    sin_b = sine_tab[:, None, :] * direction
    new_first = first_half * cos_b - second_half * sin_b
    new_second = second_half * cos_b + first_half * sin_b
    return jnp.concatenate([new_first, new_second, rest_dims], axis=-1)


def gelu_exact(pre_act):
    return 0.5 * pre_act * (1.0 + lax.erf(pre_act * (1.0 / math.sqrt(2.0))))


def gelu_slope(pre_act):
    cdf_part = 0.5 * (1.0 + lax.erf(pre_act * (1.0 / math.sqrt(2.0))))
    return cdf_part + pre_act * jnp.exp(-0.5 * pre_act * pre_act) * (1.0 / math.sqrt(2.0 * math.pi))


def per_device(
    block_input,
    cotangent,
    lengths,
    attn_gain,
    attn_shift,
    ffn_gain,
    ffn_shift,
    qkv_weight,
    qkv_bias,
    out_weight,
    out_bias,
    up_weight,
    up_bias,
    down_weight,
):
    gathered = (
        lax.all_gather(qkv_weight, "dp", axis=1, tiled=True),
        lax.all_gather(out_weight, "dp", axis=1, tiled=True),
        lax.all_gather(up_weight, "dp", axis=0, tiled=True),
        lax.all_gather(down_weight, "dp", axis=1, tiled=True),
        lax.all_gather(qkv_bias, "dp", axis=1, tiled=True),
        lax.all_gather(up_bias, "dp", axis=0, tiled=True),
        lax.all_gather(out_bias, "dp", axis=0, tiled=True),
        lax.all_gather(attn_gain, "dp", axis=0, tiled=True),
        lax.all_gather(attn_shift, "dp", axis=0, tiled=True),
        lax.all_gather(ffn_gain, "dp", axis=0, tiled=True),
        lax.all_gather(ffn_shift, "dp", axis=0, tiled=True),
    )
    (
        qkv_full,
        out_full,
        up_full,
        down_full,
        qkv_b,
        up_b,
        outb_full,
        gain_a,
        shift_a,
        gain_f,
        shift_f,
    ) = gathered
    gain_a = gain_a.astype(jnp.float32)
    gain_f = gain_f.astype(jnp.float32)
    seq_rows = block_input.shape[0]
    local_width = qkv_full.shape[2]
    local_heads = local_width // HD
    seq_len = lengths[0]
    positions = jnp.arange(seq_rows, dtype=jnp.int32)
    scale_qk = 1.0 / math.sqrt(HD)
    block_rows = min(512, seq_rows)
    x_rows = block_input.astype(jnp.float32)
    row_mean = jnp.mean(x_rows, axis=-1, keepdims=True)
    centered = x_rows - row_mean
    inv_std = lax.rsqrt(jnp.mean(centered * centered, axis=-1, keepdims=True) + norm_eps)
    normed = centered * inv_std
    attn_in = (normed * gain_a + shift_a.astype(jnp.float32)).astype(jnp.bfloat16)
    ffn_in = (normed * gain_f + shift_f.astype(jnp.float32)).astype(jnp.bfloat16)
    qkv_rows = (
        jnp.einsum("ld,pde->ple", attn_in, qkv_full, preferred_element_type=jnp.float32)
        + qkv_b.astype(jnp.float32)[:, None, :]
    )
    cosine, sine_tab = rope_tables(seq_rows, ROT)
    query_rows = rotate(
        qkv_rows[0].reshape(seq_rows, local_heads, HD), cosine, sine_tab, 1.0
    ).astype(jnp.bfloat16)
    key_rows = rotate(qkv_rows[1].reshape(seq_rows, local_heads, HD), cosine, sine_tab, 1.0).astype(
        jnp.bfloat16
    )
    value_rows = qkv_rows[2].reshape(seq_rows, local_heads, HD).astype(jnp.bfloat16)

    def block_scores(row_lo, key_end):
        raw_scores = (
            jnp.einsum("lhe,mhe->hlm", query_rows, key_rows, preferred_element_type=jnp.float32)
            * scale_qk
        )
        key_mask = (positions[None, :key_end] <= positions[row_lo:key_end, None]) & (
            positions[None, :key_end] < seq_len
        )
        return jnp.where(key_mask[None], raw_scores, -jnp.inf)

    qblock = 0
    row_lo = qblock * block_rows
    key_end = row_lo + block_rows
    scores = block_scores(row_lo, key_end)
    row_max = jnp.max(scores, axis=-1, keepdims=True)
    exp_terms = jnp.exp(scores - row_max)
    row_total = jnp.sum(exp_terms, axis=-1, keepdims=True)
    prob_bf = (exp_terms / row_total).astype(jnp.bfloat16)
    lse_blocks = [row_max + jnp.log(row_total)]
    attn_blocks = jnp.einsum(
        "hlm,mhe->lhe", prob_bf, value_rows, preferred_element_type=jnp.float32
    ).astype(jnp.bfloat16)
    mixed_flat = attn_blocks.reshape(seq_rows, local_width)
    attn_part = jnp.dot(mixed_flat, out_full, preferred_element_type=jnp.float32)
    up_pre = jnp.dot(ffn_in, up_full, preferred_element_type=jnp.float32) + up_b.astype(jnp.float32)
    hidden = gelu_exact(up_pre).astype(jnp.bfloat16)
    ffn_part = jnp.dot(hidden, down_full, preferred_element_type=jnp.float32)
    branch_sum = lax.psum(attn_part + ffn_part, "tensor")
    block_output = (x_rows + branch_sum + outb_full.astype(jnp.float32)).astype(jnp.bfloat16)
    qkv_back, out_back, up_back, down_back = (qkv_full, out_full, up_full, down_full)
    row_valid = (positions < seq_len).astype(jnp.float32)[:, None]
    grad_rows = cotangent.astype(jnp.float32) * row_valid
    grad_bf = grad_rows.astype(jnp.bfloat16)
    dout_b = jnp.sum(grad_rows, axis=0)
    ddown_w = jnp.einsum("lf,ld->fd", hidden, grad_bf, preferred_element_type=jnp.float32)
    up_grad32 = jnp.einsum(
        "ld,fd->lf", grad_bf, down_back, preferred_element_type=jnp.float32
    ) * gelu_slope(up_pre)
    up_grad = up_grad32.astype(jnp.bfloat16)
    dup_w = jnp.einsum("ld,lf->df", ffn_in, up_grad, preferred_element_type=jnp.float32)
    dup_b = jnp.sum(up_grad32, axis=0)
    ffn_back = jnp.einsum("lf,df->ld", up_grad, up_back, preferred_element_type=jnp.float32)
    mixed_grad = (
        jnp.einsum("ld,ed->le", grad_bf, out_back, preferred_element_type=jnp.float32)
        .astype(jnp.bfloat16)
        .reshape(seq_rows, local_heads, HD)
    )
    dout_w = jnp.einsum("le,ld->ed", mixed_flat, grad_bf, preferred_element_type=jnp.float32)
    delta_rows = jnp.einsum(
        "lhe,lhe->hl", mixed_grad, attn_blocks, preferred_element_type=jnp.float32
    )
    query_grad = jnp.zeros((seq_rows, local_heads, HD), jnp.float32)
    key_grad = jnp.zeros((seq_rows, local_heads, HD), jnp.float32)
    value_grad = jnp.zeros((seq_rows, local_heads, HD), jnp.float32)
    qblock = 0
    row_lo = qblock * block_rows
    key_end = row_lo + block_rows
    scores = block_scores(row_lo, key_end)
    probs32 = jnp.exp(scores - lse_blocks[qblock])
    prob_back = probs32.astype(jnp.bfloat16)
    value_grad = value_grad.at[:key_end].add(
        jnp.einsum("hlm,lhe->mhe", prob_back, mixed_grad, preferred_element_type=jnp.float32)
    )
    prob_grad = jnp.einsum(
        "lhe,mhe->hlm", mixed_grad, value_rows, preferred_element_type=jnp.float32
    )
    score_grad = (probs32 * (prob_grad - delta_rows[:, row_lo:key_end, None]) * scale_qk).astype(
        jnp.bfloat16
    )
    query_grad = query_grad.at[row_lo:key_end].set(
        jnp.einsum("hlm,mhe->lhe", score_grad, key_rows, preferred_element_type=jnp.float32)
    )
    key_grad = key_grad.at[:key_end].add(
        jnp.einsum("hlm,lhe->mhe", score_grad, query_rows, preferred_element_type=jnp.float32)
    )
    query_grad = rotate(query_grad, cosine, sine_tab, -1.0)
    key_grad = rotate(key_grad, cosine, sine_tab, -1.0)
    qkv_grad32 = jnp.stack([query_grad, key_grad, value_grad]).reshape(3, seq_rows, local_width)
    dqkv_b = jnp.sum(qkv_grad32, axis=1)
    qkv_grad = qkv_grad32.astype(jnp.bfloat16)
    dqkv_w = jnp.einsum("ld,ple->pde", attn_in, qkv_grad, preferred_element_type=jnp.float32)
    attn_back = jnp.einsum("ple,pde->ld", qkv_grad, qkv_back, preferred_element_type=jnp.float32)
    norm_part = attn_back * gain_a + ffn_back * gain_f
    norm_stats = jnp.stack(
        [
            jnp.sum(attn_back * normed, axis=0),
            jnp.sum(attn_back, axis=0),
            jnp.sum(ffn_back * normed, axis=0),
            jnp.sum(ffn_back, axis=0),
        ]
    )
    norm_grad, stat_sum = lax.psum((norm_part, norm_stats), "tensor")
    grad_mean = jnp.mean(norm_grad, axis=-1, keepdims=True)
    grad_proj = jnp.mean(norm_grad * normed, axis=-1, keepdims=True)
    dblock_input = (grad_rows + inv_std * (norm_grad - grad_mean - normed * grad_proj)).astype(
        jnp.bfloat16
    )
    dqkv_sent, dout_sent, dup_sent, ddown_sent, dqkvb_sent, dupb_sent, doutb_sent, stats_sent = (
        lax.psum_scatter(dqkv_w, "dp", scatter_dimension=1, tiled=True),
        lax.psum_scatter(dout_w, "dp", scatter_dimension=1, tiled=True),
        lax.psum_scatter(dup_w, "dp", scatter_dimension=0, tiled=True),
        lax.psum_scatter(ddown_w, "dp", scatter_dimension=1, tiled=True),
        lax.psum_scatter(dqkv_b, "dp", scatter_dimension=1, tiled=True),
        lax.psum_scatter(dup_b, "dp", scatter_dimension=0, tiled=True),
        lax.psum_scatter(dout_b, "dp", scatter_dimension=0, tiled=True),
        lax.psum_scatter(stat_sum, "dp", scatter_dimension=1, tiled=True),
    )
    return (
        block_output,
        dblock_input,
        stats_sent[0],
        stats_sent[1],
        stats_sent[2],
        stats_sent[3],
        dqkv_sent,
        dqkvb_sent,
        dout_sent,
        doutb_sent,
        dup_sent,
        dupb_sent,
        ddown_sent,
    )


def solution(mesh):
    in_specs = (
        P("dp", None),
        P("dp", None),
        P("dp"),
        P("dp"),
        P("dp"),
        P("dp"),
        P("dp"),
        P(None, "dp", "tensor"),
        P(None, ("tensor", "dp")),
        P("tensor", "dp"),
        P("dp"),
        P("dp", "tensor"),
        P(("tensor", "dp")),
        P("tensor", "dp"),
    )
    out_specs = (
        P("dp", None),
        P("dp", None),
        P("dp"),
        P("dp"),
        P("dp"),
        P("dp"),
        P(None, "dp", "tensor"),
        P(None, ("tensor", "dp")),
        P("tensor", "dp"),
        P("dp"),
        P("dp", "tensor"),
        P(("tensor", "dp")),
        P("tensor", "dp"),
    )
    return jax.shard_map(
        per_device, mesh=mesh, in_specs=in_specs, out_specs=out_specs, check_vma=False
    )
```

profile of v0, /device:TPU:0, one launch (start us, length us, event | category | flops | bytes accessed | tf_op | source)
XLA Modules:
  0.0 1075.0 jit_solution(16801075878062956087)
XLA Ops:
  12.5 13.6 %all-gather.5 = bf16[8,1,256]{2,1,0:T(2,128)(2,1)S(1)} all-gather(bf16[1,1,256]{2,1,0:T(2,128)(2,1)S(1)} %reshape.282), channel_id=1, replica_groups=mesh['dp'=8,'tensor'=4] {'dp'}, dimensions={0}, use_global_device_ids=true | all-gather | bytes 4608 | tf_op jit(solution)/shard_map/all_gather | solution.py:64
  26.7 9.0 all-gather.4
  36.3 10.3 all-gather.3
  46.6 8.8 all-gather.1
  55.4 10.4 all-gather
  65.9 17.9 %all-gather.2 = bf16[8,64,3]{1,2,0:T(4,128)(2,1)S(1)} all-gather(bf16[1,64,3]{1,2,0:T(4,128)(2,1)S(1)} %bitcast.120), channel_id=1, replica_groups=mesh['dp'=8,'tensor'=4] {'dp'}, dimensions={0}, use_global_device_ids=true | all-gather | bytes 3456 | tf_op jit(solution)/shard_map/all_gather | solution.py:63
  92.0 17.6 %all-gather.12.cloned.1.call-done = bf16[3,2048,512]{1,2,0:T(8,128)(2,1)} async-done(((bf16[3,256,512]{1,2,0:T(8,128)(2,1)}), bf16[3,2048,512]{1,2,0:T(8,128)(2,1)}) %all-gather.12.cloned.1.call-update) | async-done | bytes 6291472 | tf_op jit(solution)/shard_map/all_gather | solution.py:59
  161.2 30.2 %all-gather.16.cloned.1.call-done = bf16[2048,2048]{1,0:T(8,128)(2,1)} async-done(((bf16[256,2048]{1,0:T(8,128)(2,1)}), bf16[2048,2048]{1,0:T(8,128)(2,1)}) %all-gather.16.cloned.1.call-update) | async-done | bytes 8388624 | tf_op jit(solution)/shard_map/all_gather | solution.py:61
  191.4 9.7 fusion.53
  201.1 72.7 %all-gather.18.cloned.1.call-done = bf16[2048,2048]{1,0:T(8,128)(2,1)} async-done(((bf16[2048,256]{1,0:T(8,128)(2,1)}), bf16[2048,2048]{1,0:T(8,128)(2,1)}) %all-gather.18.cloned.1.call-update) | async-done | bytes 8388624 | tf_op jit(solution)/shard_map/all_gather | solution.py:62
  273.9 10.8 %fusion.68 = (f32[2048]{0:T(1024)S(1)}, bf16[512,2048]{1,0:T(8,128)(2,1)}) fusion(f32[512,2048]{1,0:T(8,128)} %fusion.53, f32[2048]{0:T(1024)S(1)} %bitcast.114, bf16[2048,2048]{1,0:T(8,128)(2,1)} %all-gather.18.cloned.1.call-done, bf16[512,2048]{1,0:T(8,128)(2,1)} %param.27, f32[512]{0:T(512)S(1)} %copy-done.26), kind=kOutput, calls=%fused_computation.105 | convolution fusion | flops 4310693888 | bytes 16795648 | tf_op jit(solution)/shard_map/ld,fd->lf/dot_general | solution.py:148
  284.7 8.1 fusion.61
  292.8 7.8 fusion.40
  312.6 167.7 %all-reduce.6.cloned.1.call-done = (f32[512,2048]{1,0:T(8,128)}, f32[512,2048]{1,0:T(8,128)}) async-done(((f32[512,2048]{1,0:T(8,128)}, f32[512,2048]{1,0:T(8,128)}), (f32[512,2048]{1,0:T(8,128)}, f32[512,2048]{1,0:T(8,128)})) %all-reduce.6.cloned.1.call-update) | async-done | bytes 8388624 | tf_op jit(solution)/shard_map/psum | solution.py:140
  487.8 8.4 convolution_bitcast_fusion
  502.3 13.3 %fusion.55 = f32[2048,2048]{1,0:T(8,128)} fusion(bf16[512,2048]{1,0:T(8,128)(2,1)} %param.27, f32[512]{0:T(512)S(1)} %copy-done.26, f32[512,2048]{1,0:T(8,128)} %fusion.53, f32[2048]{0:T(1024)S(1)} %bitcast.116), kind=kOutput, calls=%fused_computation.96 | convolution fusion | flops 4304404480 | bytes 23078912 | tf_op jit(solution)/shard_map/lf,ld->fd/dot_general | solution.py:147
  515.7 10.0 fusion.38
  526.3 11.8 %all-gather.6 = bf16[8,1,256]{2,1,0:T(2,128)(2,1)S(1)} all-gather(bf16[1,1,256]{2,1,0:T(2,128)(2,1)S(1)} %reshape.284), channel_id=1, replica_groups=mesh['dp'=8,'tensor'=4] {'dp'}, dimensions={0}, use_global_device_ids=true | all-gather | bytes 4608 | tf_op jit(solution)/shard_map/all_gather | solution.py:65
  547.8 27.4 %all-reduce.2 = (f32[2048]{0:T(1024)S(1)}, f32[2048]{0:T(1024)S(1)}) all-reduce(f32[2048]{0:T(1024)S(1)} %get-tuple-element.141, f32[2048]{0:T(1024)S(1)} %get-tuple-element.173), channel_id=6, replica_groups=mesh['dp'=8,'tensor'=4] {'dp'}, use_global_device_ids=true, to_apply=%region_19.20.clone | all-reduce | flops 4096 | bytes 32768
  577.5 9.5 psum.24
  587.6 90.5 %reduce-scatter.11.cloned.1.call-done = f32[3,256,512]{1,2,0:T(8,128)} async-done(((f32[3,2048,512]{1,2,0:T(8,128)}), f32[3,256,512]{1,2,0:T(8,128)}) %reduce-scatter.11.cloned.1.call-update) | async-done | bytes 1572880 | tf_op jit(solution)/shard_map/reduce_scatter | solution.py:211
  681.1 48.0 %reduce-scatter.13.cloned.1.call-done = f32[512,256]{1,0:T(8,128)} async-done(((f32[512,2048]{1,0:T(8,128)}), f32[512,256]{1,0:T(8,128)}) %reduce-scatter.13.cloned.1.call-update) | async-done | bytes 524304 | tf_op jit(solution)/shard_map/reduce_scatter | solution.py:212
  729.1 169.5 %reduce-scatter.17.cloned.1.call-done = f32[2048,256]{1,0:T(8,128)} async-done(((f32[2048,2048]{1,0:T(8,128)}), f32[2048,256]{1,0:T(8,128)}) %reduce-scatter.17.cloned.1.call-update) | async-done | bytes 2097168 | tf_op jit(solution)/shard_map/reduce_scatter | solution.py:214
  898.6 169.6 %reduce-scatter.15.cloned.1.call-done = f32[256,2048]{1,0:T(8,128)} async-done(((f32[2048,2048]{1,0:T(8,128)}), f32[256,2048]{1,0:T(8,128)}) %reduce-scatter.15.cloned.1.call-update) | async-done | bytes 2097168 | tf_op jit(solution)/shard_map/reduce_scatter | solution.py:213
  (188 shorter events, 106.4 us)
Async XLA Ops:
  7.2 58.6 %copy-start.33 = (bf16[3,64]{1,0:T(4,128)(2,1)S(1)}, bf16[3,64]{1,0:T(4,128)(2,1)}, u32[]{:S(2)}) copy-start(bf16[3,64]{1,0:T(4,128)(2,1)} %param.34) | copy-start | bytes 1156
  7.2 76.6 %copy-start = (bf16[512,2048]{1,0:T(8,128)(2,1)S(1)}, bf16[512,2048]{1,0:T(8,128)(2,1)}, u32[]{:S(2)}) copy-start(bf16[512,2048]{1,0:T(8,128)(2,1)} %param.26) | copy-start | bytes 6291460
  7.3 80.3 %all-gather.14.cloned.1.call-start = ((), (), s32[]{:S(2)}) async-start(), calls=%async_computation.7 | async-start | bytes 2359296 | tf_op jit(solution)/shard_map/all_gather | solution.py:60
  8.0 101.5 %all-gather.12.cloned.1.call-start = ((), (), s32[]{:S(2)}) async-start(), calls=%async_computation.6 | async-start | bytes 7077888 | tf_op jit(solution)/shard_map/all_gather | solution.py:59
  10.3 181.1 %all-gather.16.cloned.1.call-start = ((), (), s32[]{:S(2)}) async-start(), calls=%async_computation.8 | async-start | bytes 9437184 | tf_op jit(solution)/shard_map/all_gather | solution.py:61
  11.1 262.8 %all-gather.18.cloned.1.call-start = ((), (), s32[]{:S(2)}) async-start(), calls=%async_computation.9 | async-start | bytes 9437184 | tf_op jit(solution)/shard_map/all_gather | solution.py:62
  11.7 468.6 %all-reduce.6.cloned.1.call-start = ((), (), s32[]{:S(2)}) async-start(), calls=%async_computation.16 | async-start | bytes 16777216 | tf_op jit(solution)/shard_map/psum | solution.py:140
  55.4 54.1 %copy-start.31 = (f32[8,1,256]{2,1,0:T(1,128)}, f32[8,1,256]{2,1,0:T(1,128)S(1)}, u32[]{:S(2)}) copy-start(f32[8,1,256]{2,1,0:T(1,128)S(1)} %convert_element_type.108) | copy-start | bytes 24580
  84.2 25.3 %copy-start.23 = (f32[512]{0:T(512)}, f32[512]{0:T(512)S(1)}, u32[]{:S(2)}) copy-start(f32[512]{0:T(512)S(1)} %broadcast_multiply_fusion.3) | copy-start | bytes 6148
  84.9 24.6 %copy-start.27 = (f32[512]{0:T(512)}, f32[512]{0:T(512)S(1)}, u32[]{:S(2)}) copy-start(f32[512]{0:T(512)S(1)} %add_rsqrt_fusion) | copy-start | bytes 6148
  151.0 40.4 %copy-start.24 = (f32[512]{0:T(512)S(1)}, f32[512]{0:T(512)}, u32[]{:S(2)}) copy-start(f32[512]{0:T(512)} %copy-done.23) | copy-start | bytes 6148
  151.0 40.4 %copy-start.28 = (f32[512]{0:T(512)S(1)}, f32[512]{0:T(512)}, u32[]{:S(2)}) copy-start(f32[512]{0:T(512)} %copy-done.27) | copy-start | bytes 6148
  151.0 40.4 %copy-start.29 = (f32[8,1,256]{2,1,0:T(1,128)S(1)}, f32[8,1,256]{2,1,0:T(1,128)}, u32[]{:S(2)}) copy-start(f32[8,1,256]{2,1,0:T(1,128)} %convert_element_type.111) | copy-start | bytes 24580
  191.4 82.4 %copy-start.26 = (f32[512]{0:T(512)S(1)}, f32[512]{0:T(512)}, u32[]{:S(2)}) copy-start(f32[512]{0:T(512)} %copy-done.25) | copy-start | bytes 6148
  191.4 82.4 %copy-start.30 = (f32[8,1,256]{2,1,0:T(1,128)S(1)}, f32[8,1,256]{2,1,0:T(1,128)}, u32[]{:S(2)}) copy-start(f32[8,1,256]{2,1,0:T(1,128)} %convert_element_type.112) | copy-start | bytes 24580
  273.9 30.1 %slice-start = ((s8[6291456]{0:T(1024)(128)(4,1)}), s8[4194304]{0:T(1024)(128)(4,1)S(1)}, s32[]{:S(2)}) async-start(s8[6291456]{0:T(1024)(128)(4,1)} %bitcast.82), calls=%async_computation.17 | async-start | bytes 8388608
  284.7 19.3 %slice-start.1 = ((s8[6291456]{0:T(1024)(128)(4,1)}), s8[2097152]{0:T(1024)(128)(4,1)S(1)}, s32[]{:S(2)}) async-start(s8[6291456]{0:T(1024)(128)(4,1)} %bitcast.82), calls=%async_computation.18 | async-start | bytes 4194304
  309.8 229.6 %reduce-scatter.19.cloned.1.call-start = ((), (), s32[]{:S(2)}) async-start(), calls=%async_computation.14 | async-start | bytes 294912
  312.5 264.0 %reduce-scatter.21.cloned.1.call-start = ((), (), s32[]{:S(2)}) async-start(), calls=%async_computation.15 | async-start | bytes 1179648
  487.8 190.3 %reduce-scatter.11.cloned.1.call-start = ((), (), s32[]{:S(2)}) async-start(), calls=%async_computation.10 | async-start | bytes 14155776 | tf_op jit(solution)/shard_map/reduce_scatter | solution.py:211
  496.2 232.9 %reduce-scatter.13.cloned.1.call-start = ((), (), s32[]{:S(2)}) async-start(), calls=%async_computation.11 | async-start | bytes 4718592 | tf_op jit(solution)/shard_map/reduce_scatter | solution.py:212
  502.2 396.4 %reduce-scatter.17.cloned.1.call-start = ((), (), s32[]{:S(2)}) async-start(), calls=%async_computation.13 | async-start | bytes 18874368 | tf_op jit(solution)/shard_map/reduce_scatter | solution.py:214
  515.6 552.5 %reduce-scatter.15.cloned.1.call-start = ((), (), s32[]{:S(2)}) async-start(), calls=%async_computation.12 | async-start | bytes 18874368 | tf_op jit(solution)/shard_map/reduce_scatter | solution.py:213
  525.7 12.5 %copy-start.40 = (u32[32]{0:T(128)S(1)}, u32[32]{0:T(128)}, u32[]{:S(2)}) copy-start(u32[32]{0:T(128)} %constant.135) | copy-start | bytes 388
  (31 other events, 130.7 us)
Sparse Core Ops, SparseCore 0:
  9.6 33.4 all-gather.13
  45.3 64.2 all-gather.11
  111.1 80.2 all-gather.15
  192.8 80.9 all-gather.17
  309.9 170.2 all-reduce.5
  482.9 31.4 reduce-scatter.18
  517.3 30.7 reduce-scatter.20
  550.4 127.6 reduce-scatter.10
  680.9 48.1 reduce-scatter.12
  731.9 166.6 reduce-scatter.16
  901.5 166.6 reduce-scatter.14
where the time goes:
time: 1080 us; the launch traced here: 1070 us
  waiting for transfers between devices  768 us (71%)
  blocking collectives  119 us (11%)
  matrix products  103 us (10%)
  local copies, waits for them, and re-layouts  44.3 us (4%)
  other arithmetic  24.7 us (2%)
  between operations  16.1 us (1%)
    reduce_scatter x1, waiting for transfers between devices, per_device(): lax.psum_scatter(dup_w, 'dp', scatter_dimension=0, tiled=True)  170 us
    reduce_scatter x1, waiting for transfers between devices, per_device(): lax.psum_scatter(ddown_w, 'dp', scatter_dimension=1, tiled=True)  169 us
    psum x1, waiting for transfers between devices, per_device(): branch_sum = lax.psum(attn_part + ffn_part, 'tensor')  168 us
    reduce_scatter x1, waiting for transfers between devices, per_device(): lax.psum_scatter(dqkv_w, 'dp', scatter_dimension=1, tiled=True)  90.5 us
    all_gather x1, waiting for transfers between devices, per_device(): lax.all_gather(down_weight, 'dp', axis=1, tiled=True)  72.7 us
    reduce_scatter x1, waiting for transfers between devices, per_device(): lax.psum_scatter(dout_w, 'dp', scatter_dimension=1, tiled=True)  48 us
    all_gather x1, waiting for transfers between devices, per_device(): lax.all_gather(up_weight, 'dp', axis=0, tiled=True)  30.2 us
    unnamed x1, blocking collectives  27.4 us
  transfers between devices with their start and end apart: 11, of which 8 were waited for; matrix products, arithmetic and copies ran while one was open for 12% of the time, Pallas kernels for 0%

commit v1 on v0

--- a/solution.py
+++ b/solution.py
@@ -8,6 +8,7 @@
 ROT = 64
 norm_eps = 1e-05
 rope_base = 10000.0
+assign_quarters_in = lambda mine_x: jnp.sum(lax.all_gather(mine_x, axis_name="tensor"), 0)
 
 
 def rope_tables(row_count, rot_width):
@@ -137,7 +138,7 @@
     up_pre = jnp.dot(ffn_in, up_full, preferred_element_type=jnp.float32) + up_b.astype(jnp.float32)
     hidden = gelu_exact(up_pre).astype(jnp.bfloat16)
     ffn_part = jnp.dot(hidden, down_full, preferred_element_type=jnp.float32)
-    branch_sum = lax.psum(attn_part + ffn_part, "tensor")
+    branch_sum = assign_quarters_in(attn_part + ffn_part)
     block_output = (x_rows + branch_sum + outb_full.astype(jnp.float32)).astype(jnp.bfloat16)
     qkv_back, out_back, up_back, down_back = (qkv_full, out_full, up_full, down_full)
     row_valid = (positions < seq_len).astype(jnp.float32)[:, None]

time: 1080 us -> 1160 us (1.074)
  waiting for transfers between devices: 768 us -> 835 us
    all_gather x0 -> x1, waiting for transfers between devices: none -> 155 us  [lax.all_gather(mine_x, axis_name='tensor')]
    psum x1, waiting for transfers between devices: 168 us -> 99.3 us  [per_device(): norm_grad, stat_sum = lax.psum((norm_part, norm_stats), 'tensor')]
    reduce_scatter x1, waiting for transfers between devices: 48 us -> 4.96 us  [per_device(): lax.psum_scatter(dout_w, 'dp', scatter_dimension=1, tiled=True)]
    reduce_scatter x1, waiting for transfers between devices: 90.5 us -> 113 us  [per_device(): lax.psum_scatter(dqkv_w, 'dp', scatter_dimension=1, tiled=True)]
    unnamed x109 -> x105, local copies, waits for them, and re-layouts: 24.1 us -> 22.3 us
  transfers between devices with their start and end apart: 11 -> 12, of which waited for: 8 -> 9; matrix products, arithmetic and copies ran while one was open for 12% -> 13% of each run, Pallas kernels for 0% -> 0%
where the time goes in v1:
time: 1160 us; the launch traced here: 1150 us
  waiting for transfers between devices  835 us (72%)
  blocking collectives  121 us (10%)
  matrix products  104 us (9%)
  local copies, waits for them, and re-layouts  42.5 us (4%)
  other arithmetic  34.3 us (3%)
  between operations  16.3 us (1%)
    reduce_scatter x1, waiting for transfers between devices, per_device(): lax.psum_scatter(dup_w, 'dp', scatter_dimension=0, tiled=True)  170 us
    reduce_scatter x1, waiting for transfers between devices, per_device(): lax.psum_scatter(ddown_w, 'dp', scatter_dimension=1, tiled=True)  169 us
    all_gather x1, waiting for transfers between devices, lax.all_gather(mine_x, axis_name='tensor')  155 us
    reduce_scatter x1, waiting for transfers between devices, per_device(): lax.psum_scatter(dqkv_w, 'dp', scatter_dimension=1, tiled=True)  113 us
    psum x1, waiting for transfers between devices, per_device(): norm_grad, stat_sum = lax.psum((norm_part, norm_stats), 'tensor')  99.3 us
    all_gather x1, waiting for transfers between devices, per_device(): lax.all_gather(down_weight, 'dp', axis=1, tiled=True)  72.8 us
    all_gather x1, waiting for transfers between devices, per_device(): lax.all_gather(up_weight, 'dp', axis=0, tiled=True)  31.5 us
    unnamed x1, blocking collectives  30.2 us
  transfers between devices with their start and end apart: 12, of which 9 were waited for; matrix products, arithmetic and copies ran while one was open for 13% of the time, Pallas kernels for 0%

profile of v1, /device:TPU:0, one launch (start us, length us, event | category | flops | bytes accessed | tf_op | source)
XLA Modules:
  0.0 1153.9 jit_solution(10238605082262000953)
XLA Ops:
  12.4 13.6 %all-gather.5 = bf16[8,1,256]{2,1,0:T(2,128)(2,1)S(1)} all-gather(bf16[1,1,256]{2,1,0:T(2,128)(2,1)S(1)} %reshape.281), channel_id=1, replica_groups=mesh['dp'=8,'tensor'=4] {'dp'}, dimensions={0}, use_global_device_ids=true | all-gather | bytes 4608 | tf_op jit(solution)/shard_map/all_gather | solution.py:70
  26.6 9.0 all-gather.4
  35.6 10.4 all-gather.6
  46.6 8.7 all-gather.1
  55.4 10.5 all-gather.3
  66.0 17.9 %all-gather.2 = bf16[8,1,256]{2,1,0:T(2,128)(2,1)S(1)} all-gather(bf16[1,1,256]{2,1,0:T(2,128)(2,1)S(1)} %reshape.275), channel_id=1, replica_groups=mesh['dp'=8,'tensor'=4] {'dp'}, dimensions={0}, use_global_device_ids=true | all-gather | bytes 4608 | tf_op jit(solution)/shard_map/all_gather | solution.py:68
  91.9 17.6 %all-gather.14.cloned.1.call-done = bf16[3,2048,512]{1,2,0:T(8,128)(2,1)} async-done(((bf16[3,256,512]{1,2,0:T(8,128)(2,1)}), bf16[3,2048,512]{1,2,0:T(8,128)(2,1)}) %all-gather.14.cloned.1.call-update) | async-done | bytes 6291472 | tf_op jit(solution)/shard_map/all_gather | solution.py:60
  159.9 31.5 %all-gather.18.cloned.1.call-done = bf16[2048,2048]{1,0:T(8,128)(2,1)} async-done(((bf16[256,2048]{1,0:T(8,128)(2,1)}), bf16[2048,2048]{1,0:T(8,128)(2,1)}) %all-gather.18.cloned.1.call-update) | async-done | bytes 8388624 | tf_op jit(solution)/shard_map/all_gather | solution.py:62
  191.5 9.6 fusion.53
  201.1 72.8 %all-gather.20.cloned.1.call-done = bf16[2048,2048]{1,0:T(8,128)(2,1)} async-done(((bf16[2048,256]{1,0:T(8,128)(2,1)}), bf16[2048,2048]{1,0:T(8,128)(2,1)}) %all-gather.20.cloned.1.call-update) | async-done | bytes 8388624 | tf_op jit(solution)/shard_map/all_gather | solution.py:63
  273.9 9.9 fusion.68
  288.4 10.3 fusion.27
  301.4 99.3 %all-reduce.5.cloned.1.call-done = f32[512,2048]{1,0:T(8,128)} async-done(((f32[512,2048]{1,0:T(8,128)}), f32[512,2048]{1,0:T(8,128)}) %all-reduce.5.cloned.1.call-update) | async-done | bytes 4194320 | tf_op jit(solution)/shard_map/psum | solution.py:205
  416.9 9.3 fusion.61
  434.7 10.0 fusion.38
  444.9 13.4 %fusion.55 = f32[2048,2048]{1,0:T(8,128)} fusion(bf16[512,2048]{1,0:T(8,128)(2,1)} %param.27, f32[512]{0:T(512)S(1)} %copy-done.25, f32[512,2048]{1,0:T(8,128)} %fusion.53, f32[2048]{0:T(1024)S(1)} %bitcast.114), kind=kOutput, calls=%fused_computation.96 | convolution fusion | flops 4304404480 | bytes 23078912 | tf_op jit(solution)/shard_map/lf,ld->fd/dot_general | solution.py:148
  459.0 11.8 %all-gather.7 = bf16[8,1,256]{2,1,0:T(2,128)(2,1)S(1)} all-gather(bf16[1,1,256]{2,1,0:T(2,128)(2,1)S(1)} %reshape.285), channel_id=1, replica_groups=mesh['dp'=8,'tensor'=4] {'dp'}, dimensions={0}, use_global_device_ids=true | all-gather | bytes 4608 | tf_op jit(solution)/shard_map/all_gather | solution.py:66
  474.5 8.9 psum.16
  484.0 112.9 %reduce-scatter.11.cloned.1.call-done = f32[3,256,512]{1,2,0:T(8,128)} async-done(((f32[3,2048,512]{1,2,0:T(8,128)}), f32[3,256,512]{1,2,0:T(8,128)}) %reduce-scatter.11.cloned.1.call-update) | async-done | bytes 1572880 | tf_op jit(solution)/shard_map/reduce_scatter | solution.py:212
  599.9 154.6 %all-gather.22.cloned.1.call-done = f32[2048,2048]{1,0:T(8,128)} async-done(((f32[512,2048]{1,0:T(8,128)}), f32[2048,2048]{1,0:T(8,128)}) %all-gather.22.cloned.1.call-update) | async-done | bytes 16777232 | tf_op jit(solution)/shard_map/all_gather | solution.py:11
  754.5 10.2 reduce_sum.120
  771.4 30.2 %all-reduce.2 = (f32[2048]{0:T(1024)S(1)}, f32[2048]{0:T(1024)S(1)}) all-reduce(f32[2048]{0:T(1024)S(1)} %get-tuple-element.139, f32[2048]{0:T(1024)S(1)} %get-tuple-element.171), channel_id=7, replica_groups=mesh['dp'=8,'tensor'=4] {'dp'}, use_global_device_ids=true, to_apply=%region_19.20.clone | all-reduce | flops 4096 | bytes 32768
  807.8 169.6 %reduce-scatter.15.cloned.1.call-done = f32[256,2048]{1,0:T(8,128)} async-done(((f32[2048,2048]{1,0:T(8,128)}), f32[256,2048]{1,0:T(8,128)}) %reduce-scatter.15.cloned.1.call-update) | async-done | bytes 2097168 | tf_op jit(solution)/shard_map/reduce_scatter | solution.py:214
  977.4 169.5 %reduce-scatter.17.cloned.1.call-done = f32[2048,256]{1,0:T(8,128)} async-done(((f32[2048,2048]{1,0:T(8,128)}), f32[2048,256]{1,0:T(8,128)}) %reduce-scatter.17.cloned.1.call-update) | async-done | bytes 2097168 | tf_op jit(solution)/shard_map/reduce_scatter | solution.py:215
  (187 shorter events, 116.3 us)
Async XLA Ops:
  7.2 28.4 %copy-start.36 = (bf16[256]{0:T(256)(128)(2,1)S(1)}, bf16[256]{0:T(256)(128)(2,1)}, u32[]{:S(2)}) copy-start(bf16[256]{0:T(256)(128)(2,1)} %param.38) | copy-start | bytes 1540
  7.2 39.4 %copy-start.37 = (bf16[256]{0:T(256)(128)(2,1)S(1)}, bf16[256]{0:T(256)(128)(2,1)}, u32[]{:S(2)}) copy-start(bf16[256]{0:T(256)(128)(2,1)} %param.29) | copy-start | bytes 1540
  7.2 48.2 %copy-start.32 = (bf16[3,64]{1,0:T(4,128)(2,1)S(1)}, bf16[3,64]{1,0:T(4,128)(2,1)}, u32[]{:S(2)}) copy-start(bf16[3,64]{1,0:T(4,128)(2,1)} %param.34) | copy-start | bytes 1156
  7.2 58.7 %copy-start.38 = (bf16[256]{0:T(256)(128)(2,1)S(1)}, bf16[256]{0:T(256)(128)(2,1)}, u32[]{:S(2)}) copy-start(bf16[256]{0:T(256)(128)(2,1)} %param.30) | copy-start | bytes 1540
  7.2 76.6 %copy-start = (bf16[512,2048]{1,0:T(8,128)(2,1)S(1)}, bf16[512,2048]{1,0:T(8,128)(2,1)}, u32[]{:S(2)}) copy-start(bf16[512,2048]{1,0:T(8,128)(2,1)} %param.26) | copy-start | bytes 6291460
  7.3 80.3 %all-gather.16.cloned.1.call-start = ((), (), s32[]{:S(2)}) async-start(), calls=%async_computation.7 | async-start | bytes 2359296 | tf_op jit(solution)/shard_map/all_gather | solution.py:61
  8.0 101.5 %all-gather.14.cloned.1.call-start = ((), (), s32[]{:S(2)}) async-start(), calls=%async_computation.6 | async-start | bytes 7077888 | tf_op jit(solution)/shard_map/all_gather | solution.py:60
  10.3 181.1 %all-gather.18.cloned.1.call-start = ((), (), s32[]{:S(2)}) async-start(), calls=%async_computation.8 | async-start | bytes 9437184 | tf_op jit(solution)/shard_map/all_gather | solution.py:62
  11.1 262.8 %all-gather.20.cloned.1.call-start = ((), (), s32[]{:S(2)}) async-start(), calls=%async_computation.9 | async-start | bytes 9437184 | tf_op jit(solution)/shard_map/all_gather | solution.py:63
  11.7 389.0 %all-reduce.5.cloned.1.call-start = ((), (), s32[]{:S(2)}) async-start(), calls=%async_computation.10 | async-start | bytes 8388608 | tf_op jit(solution)/shard_map/psum | solution.py:205
  83.8 25.7 %copy-start.30 = (f32[8,1,256]{2,1,0:T(1,128)}, f32[8,1,256]{2,1,0:T(1,128)S(1)}, u32[]{:S(2)}) copy-start(f32[8,1,256]{2,1,0:T(1,128)S(1)} %convert_element_type.108) | copy-start | bytes 24580
  84.2 25.3 %copy-start.22 = (f32[512]{0:T(512)}, f32[512]{0:T(512)S(1)}, u32[]{:S(2)}) copy-start(f32[512]{0:T(512)S(1)} %broadcast_multiply_fusion.3) | copy-start | bytes 6148
  149.7 41.7 %copy-start.23 = (f32[512]{0:T(512)S(1)}, f32[512]{0:T(512)}, u32[]{:S(2)}) copy-start(f32[512]{0:T(512)} %copy-done.22) | copy-start | bytes 6148
  149.7 41.7 %copy-start.27 = (f32[512]{0:T(512)S(1)}, f32[512]{0:T(512)}, u32[]{:S(2)}) copy-start(f32[512]{0:T(512)} %copy-done.26) | copy-start | bytes 6148
  149.7 41.7 %copy-start.29 = (f32[8,1,256]{2,1,0:T(1,128)S(1)}, f32[8,1,256]{2,1,0:T(1,128)}, u32[]{:S(2)}) copy-start(f32[8,1,256]{2,1,0:T(1,128)} %convert_element_type.111) | copy-start | bytes 24580
  191.4 82.4 %copy-start.25 = (f32[512]{0:T(512)S(1)}, f32[512]{0:T(512)}, u32[]{:S(2)}) copy-start(f32[512]{0:T(512)} %copy-done.24) | copy-start | bytes 6148
  191.4 82.4 %copy-start.28 = (f32[8,1,256]{2,1,0:T(1,128)S(1)}, f32[8,1,256]{2,1,0:T(1,128)}, u32[]{:S(2)}) copy-start(f32[8,1,256]{2,1,0:T(1,128)} %convert_element_type.112) | copy-start | bytes 24580
  298.7 173.4 %reduce-scatter.19.cloned.1.call-start = ((), (), s32[]{:S(2)}) async-start(), calls=%async_computation.16 | async-start | bytes 294912
  301.4 172.1 %reduce-scatter.21.cloned.1.call-start = ((), (), s32[]{:S(2)}) async-start(), calls=%async_computation.17 | async-start | bytes 1179648
  408.1 188.8 %reduce-scatter.11.cloned.1.call-start = ((), (), s32[]{:S(2)}) async-start(), calls=%async_computation.11 | async-start | bytes 14155776 | tf_op jit(solution)/shard_map/reduce_scatter | solution.py:212
  416.9 337.7 %all-gather.22.cloned.1.call-start = ((), (), s32[]{:S(2)}) async-start(), calls=%async_computation.15 | async-start | bytes 20971520 | tf_op jit(solution)/shard_map/all_gather | solution.py:11
  429.7 378.1 %reduce-scatter.13.cloned.1.call-start = ((), (), s32[]{:S(2)}) async-start(), calls=%async_computation.12 | async-start | bytes 4718592 | tf_op jit(solution)/shard_map/reduce_scatter | solution.py:213
  434.7 542.7 %reduce-scatter.15.cloned.1.call-start = ((), (), s32[]{:S(2)}) async-start(), calls=%async_computation.13 | async-start | bytes 18874368 | tf_op jit(solution)/shard_map/reduce_scatter | solution.py:214
  444.7 702.2 %reduce-scatter.17.cloned.1.call-start = ((), (), s32[]{:S(2)}) async-start(), calls=%async_computation.14 | async-start | bytes 18874368 | tf_op jit(solution)/shard_map/reduce_scatter | solution.py:215
  (30 other events, 180.7 us)
Sparse Core Ops, SparseCore 0:
  9.6 33.4 all-gather.15
  45.3 64.2 all-gather.13
  111.1 80.2 all-gather.17
  192.9 80.9 all-gather.19
  298.8 101.8 all-reduce.4
  402.8 30.8 reduce-scatter.18
  436.5 30.7 reduce-scatter.20
  469.6 127.2 reduce-scatter.10
  598.7 155.7 all-gather.21
  757.3 50.5 reduce-scatter.12
  810.7 166.6 reduce-scatter.14
  980.2 166.6 reduce-scatter.16
